TPU v7x, 128 devices: a whole 4x4x4 slice. The times are simulated.
128 devices in a mesh: row: 8 (over y, x_lo), col: 16 (over x_hi, z, core).
Axes of the slice: x: 4 (x_hi: 2, x_lo: 2; x = x_hi * 2 + x_lo), y: 4, z: 4, core: 2. Of those that a mesh axis runs over, the one named last changes fastest.
Arguments:
- patches: bfloat16 [64, 128, 768], P('row', 'col'), may hold values from -6 to 6
- w_patch: bfloat16 [768, 6144], replicated, may hold values from -0.21875 to 0.21875
- patch_bias: bfloat16 [6144], replicated, may hold values from -5 to 5
- ln_gain: bfloat16 [6144], replicated, may hold values from 0.5 to 1.5
- w_qkv: bfloat16 [6144, 3, 48, 128], P(None, None, 'col'), may hold values from -1 to 1
- qk_gain: float32 [2, 48, 128], P(None, 'col'), may hold values from 0 to 6, as said below
- w_out: bfloat16 [48, 128, 6144], P('col', None, 'row'), may hold values from -0.078125 to 0.078125
Outputs:
- attn_branch: bfloat16 [8192, 6144], P(('row', 'col'))
Inputs may be any that keep to these rules, and one draw needn't show every extreme that they name: `qk_gain`: positive gains.
All inputs are finite; a program needn't handle non-finite values.
Results may differ from a plain program's by a relative error of at most 0.015.
Values may be sent and summed in bfloat16 or wider, within the bound.
A program may use at most 320 MiB of HBM per device.

v0:
```python
import math
import jax
import jax.numpy as jnp
from jax import lax
from jax.sharding import PartitionSpec as P

NORM_EPS = 1e-06


def sincos_table(row_ids, col_ids, model_width):
    quarter = model_width // 4
    frequency = 1.0 / 10000.0 ** (jnp.arange(quarter, dtype=jnp.float32) / quarter)
    row_angle = row_ids.astype(jnp.float32)[:, None] * frequency[None, :]
    col_angle = col_ids.astype(jnp.float32)[:, None] * frequency[None, :]
    return jnp.concatenate(
        [jnp.sin(row_angle), jnp.cos(row_angle), jnp.sin(col_angle), jnp.cos(col_angle)], axis=1
    )


def layer_norm(values, gain_row):
    mean_val = jnp.mean(values, axis=-1, keepdims=True)
    centered = values - mean_val
    variance = jnp.mean(centered * centered, axis=-1, keepdims=True)
    return centered * lax.rsqrt(variance + NORM_EPS) * gain_row


def local(patches, w_patch, patch_bias, ln_gain, w_qkv, qk_gain, w_out):
    tile_rows, tile_cols, pixel_width = patches.shape
    model_width = w_patch.shape[1]
    heads_here = w_qkv.shape[2]
    head_size = w_qkv.shape[3]
    col_count = lax.axis_size("col")
    block_tokens = tile_rows * tile_cols * col_count
    row_anchor = lax.axis_index("row") * tile_rows
    qkv_matrix = w_qkv.reshape(model_width, 3 * heads_here * head_size)
    bias_row = patch_bias.astype(jnp.float32)[None, :]
    gain_row = ln_gain.astype(jnp.float32)
    piece_cols = patches.shape[1]
    local_rows = jnp.repeat(jnp.arange(tile_rows, dtype=jnp.int32), piece_cols)
    local_cols = jnp.tile(jnp.arange(piece_cols, dtype=jnp.int32), tile_rows)
    flat_pixels = patches.reshape(tile_rows * piece_cols, pixel_width)
    embedded = jnp.dot(flat_pixels, w_patch, preferred_element_type=jnp.float32) + bias_row
    embedded = embedded + sincos_table(
        row_anchor + local_rows, lax.axis_index("col") * tile_cols + local_cols, model_width
    )
    normed = layer_norm(embedded, gain_row).astype(jnp.bfloat16)
    own_tile = normed.reshape(tile_rows, piece_cols, model_width)
    normed_piece = lax.all_gather(own_tile, "col", axis=1, tiled=True)
    piece_cols = normed_piece.shape[1]
    flat_normed = normed_piece.reshape(tile_rows * piece_cols, model_width)
    projected = jnp.dot(flat_normed, qkv_matrix, preferred_element_type=jnp.float32)
    projected = projected.reshape(tile_rows, piece_cols, 3 * heads_here * head_size)
    projected = projected.reshape(block_tokens, 3, heads_here, head_size)
    queries = layer_norm(projected[:, 0], qk_gain[0]).astype(jnp.bfloat16)
    keys_here = layer_norm(projected[:, 1], qk_gain[1]).astype(jnp.bfloat16)
    values_here = projected[:, 2].astype(jnp.bfloat16)
    query_heads = queries.transpose(1, 0, 2)
    scale_factor = 1.0 / math.sqrt(head_size)
    start_state = (
        jnp.full((heads_here, block_tokens), -1e30, jnp.float32),
        jnp.zeros((heads_here, block_tokens), jnp.float32),
        jnp.zeros((heads_here, block_tokens, head_size), jnp.float32),
    )
    key_piece = lax.all_gather(keys_here, "row", axis=0, tiled=True)
    value_piece = lax.all_gather(values_here, "row", axis=0, tiled=True)
    piece_len = key_piece.shape[0]
    key_block = math.gcd(piece_len, 1024)
    block_count = piece_len // key_block
    key_blocks = key_piece.reshape(block_count, key_block, heads_here, head_size)
    value_blocks = value_piece.reshape(block_count, key_block, heads_here, head_size)

    def step_block(state, block_args):
        run_peak, run_total, run_acc = state
        block_keys, block_values = block_args
        scores = (
            jnp.einsum("hqd,khd->hqk", query_heads, block_keys, preferred_element_type=jnp.float32)
            * scale_factor
        )
        new_peak = jnp.maximum(run_peak, jnp.max(scores, axis=2))
        rescale = jnp.exp(run_peak - new_peak)
        exponent = jnp.exp(scores - new_peak[:, :, None])
        new_total = run_total * rescale + jnp.sum(exponent, axis=2)
        weighted = jnp.einsum(
            "hqk,khd->hqd",
            exponent.astype(jnp.bfloat16),
            block_values,
            preferred_element_type=jnp.float32,
        )
        new_acc = run_acc * rescale[:, :, None] + weighted
        return ((new_peak, new_total, new_acc), None)

    final_state, unused = lax.scan(step_block, start_state, (key_blocks, value_blocks))
    peak_all, total_all, acc_all = final_state
    context = (acc_all / total_all[:, :, None]).astype(jnp.bfloat16)
    context = context.transpose(1, 0, 2).reshape(block_tokens, heads_here * head_size)
    out_weight = lax.all_gather(w_out, "row", axis=2, tiled=True).reshape(
        heads_here * head_size, model_width
    )
    return lax.psum_scatter(
        jnp.dot(context, out_weight, preferred_element_type=jnp.float32).astype(jnp.bfloat16),
        "col",
        scatter_dimension=0,
        tiled=True,
    )


def solution(mesh):
    return jax.shard_map(
        local,
        mesh=mesh,
        in_specs=(
            P("row", "col", None),
            P(),
            P(),
            P(),
            P(None, None, "col", None),
            P(None, "col", None),
            P("col", None, "row"),
        ),
        out_specs=P(("row", "col"), None),
        check_vma=False,
    )
```

profile of v0, /device:TPU:0, one launch (start us, length us, event | category | flops | bytes accessed | tf_op | source)
XLA Modules:
  0.0 726.4 jit_solution(8967606610263915652)
XLA Ops:
  10.3 5.6 fusion.27
  17.8 18.8 %copy.13 = bf16[6144,3,3,128]{0,3,2,1:T(8,128)(2,1)} copy(bf16[6144,3,3,128]{3,0,2,1:T(8,128)(2,1)} %param.13) | data formatting | bytes 28311552 | tf_op args[4]
  36.6 74.4 %all-gather.6.cloned.1.call-done = bf16[8,128,6144]{2,1,0:T(8,128)(2,1)} async-done(((bf16[8,8,6144]{2,1,0:T(8,128)(2,1)}), bf16[8,128,6144]{2,1,0:T(8,128)(2,1)}) %all-gather.6.cloned.1.call-update) | async-done | bytes 12582928 | tf_op jit(solution)/shard_map/all_gather | solution.py:48
  110.9 19.3 %fusion.19 = f32[1024,3,3,128]{0,3,2,1:T(8,128)S(1)} fusion(bf16[1024,6144,1,1]{1,0,3,2:T(8,128)(2,1)} %bitcast.97, bf16[6144,3,3,128]{0,3,2,1:T(8,128)(2,1)} %copy.13), kind=kOutput, calls=%fused_computation.23 | convolution fusion | flops 14495514624 | bytes 31457280 | tf_op jit(solution)/shard_map/dot_general | solution.py:51
  138.2 122.7 %all-gather.8.cloned.1.call-done = bf16[8192,3,128]{0,2,1:T(8,128)(2,1)} async-done(((bf16[1024,3,128]{0,2,1:T(8,128)(2,1)}), bf16[8192,3,128]{0,2,1:T(8,128)(2,1)}) %all-gather.8.cloned.1.call-update) | async-done | bytes 6291472 | tf_op jit(solution)/shard_map/all_gather | solution.py:64
  260.9 12.7 %copy.21 = bf16[48,8,8,1024]{3,2,1,0:T(8,128)(2,1)} copy(bf16[48,8,8,1024]{3,1,2,0:T(8,128)(2,1)} %bitcast.95) | data formatting | bytes 12582912
  273.6 9.1 %copy.14 = bf16[8,1024,3,128]{3,1,2,0:T(8,128)(2,1)} copy(bf16[8,1024,3,128]{1,0,3,2:T(8,128)(2,1)} %bitcast.93) | data formatting | bytes 12582912
  282.8 109.8 %all-gather.12.cloned.1.call-done = bf16[8192,1,3,128]{0,3,2,1:T(8,128)(2,1)} async-done(((bf16[1024,1,3,128]{0,3,2,1:T(8,128)(2,1)}), bf16[8192,1,3,128]{0,3,2,1:T(8,128)(2,1)}) %all-gather.12.cloned.1.call-update) | async-done | bytes 6291472 | tf_op jit(solution)/shard_map/all_gather | solution.py:65
  392.6 12.7 %copy.22 = bf16[48,8,8,1024]{3,2,1,0:T(8,128)(2,1)} copy(bf16[48,8,8,1024]{3,1,2,0:T(8,128)(2,1)} %bitcast.96) | data formatting | bytes 12582912
  405.3 9.2 %copy.16 = bf16[8,1024,3,128]{3,1,2,0:T(8,128)(2,1)} copy(bf16[8,1024,3,128]{1,0,3,2:T(8,128)(2,1)} %bitcast.94) | data formatting | bytes 12582912
  414.5 170.3 %while.15 = (s32[]{:T(128)}, f32[3,1024]{1,0:T(4,128)S(1)}, f32[3,1024]{1,0:T(4,128)S(1)}, f32[3,1024,128]{2,1,0:T(8,128)}, bf16[8,1024,3,128]{3,1,2,0:T(8,128)(...) while((s32[]{:T(128)}, f32[3,1024]{1,0:T(4,128)S(1)}, ...), condition=%wide.region_9.10_spmd.clone, body=%wide.region_6.9_spmd.clone.sunk | while | flops 1636973568 | bytes 93783168 | solution.py:92
  414.5 7.7 %bitcast_reduce_fusion.2 = (f32[3,1024]{1,0:T(4,128)S(1)}, f32[3,1024,1024]{2,1,0:T(8,128)}) fusion(bf16[3,1024,128]{2,1,0:T(8,128)(2,1)} %get-tuple-element.195, bf16[8,1024,3,128]{3,1,2,0:T(8,128)(2,1)} %get-tuple-element.194, s32[]{:T(128)} %get-tuple-element.181), kind=kOutput, calls=%fused_computation.1.clone.1 | convolution fusion | flops 811594752 | bytes 14168576 | tf_op jit(solution)/shard_map/while/body/eval_jaxpr/hqd,khd->hqk/dot_general | solution.py:76
  422.3 6.9 fusion.41
  435.7 7.7 %bitcast_reduce_fusion.2 = (f32[3,1024]{1,0:T(4,128)S(1)}, f32[3,1024,1024]{2,1,0:T(8,128)}) fusion(bf16[3,1024,128]{2,1,0:T(8,128)(2,1)} %get-tuple-element.195, bf16[8,1024,3,128]{3,1,2,0:T(8,128)(2,1)} %get-tuple-element.194, s32[]{:T(128)} %get-tuple-element.181), kind=kOutput, calls=%fused_computation.1.clone.1 | convolution fusion | flops 811594752 | bytes 14168576 | tf_op jit(solution)/shard_map/while/body/eval_jaxpr/hqd,khd->hqk/dot_general | solution.py:76
  443.5 6.8 fusion.41
  451.7 5.4 fusion.43
  457.1 7.8 %bitcast_reduce_fusion.2 = (f32[3,1024]{1,0:T(4,128)S(1)}, f32[3,1024,1024]{2,1,0:T(8,128)}) fusion(bf16[3,1024,128]{2,1,0:T(8,128)(2,1)} %get-tuple-element.195, bf16[8,1024,3,128]{3,1,2,0:T(8,128)(2,1)} %get-tuple-element.194, s32[]{:T(128)} %get-tuple-element.181), kind=kOutput, calls=%fused_computation.1.clone.1 | convolution fusion | flops 811594752 | bytes 14168576 | tf_op jit(solution)/shard_map/while/body/eval_jaxpr/hqd,khd->hqk/dot_general | solution.py:76
  464.9 6.8 fusion.41
  473.1 5.4 fusion.43
  478.5 7.7 %bitcast_reduce_fusion.2 = (f32[3,1024]{1,0:T(4,128)S(1)}, f32[3,1024,1024]{2,1,0:T(8,128)}) fusion(bf16[3,1024,128]{2,1,0:T(8,128)(2,1)} %get-tuple-element.195, bf16[8,1024,3,128]{3,1,2,0:T(8,128)(2,1)} %get-tuple-element.194, s32[]{:T(128)} %get-tuple-element.181), kind=kOutput, calls=%fused_computation.1.clone.1 | convolution fusion | flops 811594752 | bytes 14168576 | tf_op jit(solution)/shard_map/while/body/eval_jaxpr/hqd,khd->hqk/dot_general | solution.py:76
  486.3 6.8 fusion.41
  494.4 5.4 fusion.43
  499.8 7.7 %bitcast_reduce_fusion.2 = (f32[3,1024]{1,0:T(4,128)S(1)}, f32[3,1024,1024]{2,1,0:T(8,128)}) fusion(bf16[3,1024,128]{2,1,0:T(8,128)(2,1)} %get-tuple-element.195, bf16[8,1024,3,128]{3,1,2,0:T(8,128)(2,1)} %get-tuple-element.194, s32[]{:T(128)} %get-tuple-element.181), kind=kOutput, calls=%fused_computation.1.clone.1 | convolution fusion | flops 811594752 | bytes 14168576 | tf_op jit(solution)/shard_map/while/body/eval_jaxpr/hqd,khd->hqk/dot_general | solution.py:76
  507.5 6.8 fusion.41
  521.0 7.7 %bitcast_reduce_fusion.2 = (f32[3,1024]{1,0:T(4,128)S(1)}, f32[3,1024,1024]{2,1,0:T(8,128)}) fusion(bf16[3,1024,128]{2,1,0:T(8,128)(2,1)} %get-tuple-element.195, bf16[8,1024,3,128]{3,1,2,0:T(8,128)(2,1)} %get-tuple-element.194, s32[]{:T(128)} %get-tuple-element.181), kind=kOutput, calls=%fused_computation.1.clone.1 | convolution fusion | flops 811594752 | bytes 14168576 | tf_op jit(solution)/shard_map/while/body/eval_jaxpr/hqd,khd->hqk/dot_general | solution.py:76
  528.8 6.8 fusion.41
  542.3 7.7 %bitcast_reduce_fusion.2 = (f32[3,1024]{1,0:T(4,128)S(1)}, f32[3,1024,1024]{2,1,0:T(8,128)}) fusion(bf16[3,1024,128]{2,1,0:T(8,128)(2,1)} %get-tuple-element.195, bf16[8,1024,3,128]{3,1,2,0:T(8,128)(2,1)} %get-tuple-element.194, s32[]{:T(128)} %get-tuple-element.181), kind=kOutput, calls=%fused_computation.1.clone.1 | convolution fusion | flops 811594752 | bytes 14168576 | tf_op jit(solution)/shard_map/while/body/eval_jaxpr/hqd,khd->hqk/dot_general | solution.py:76
  550.1 6.8 fusion.41
  563.6 7.7 %bitcast_reduce_fusion.2 = (f32[3,1024]{1,0:T(4,128)S(1)}, f32[3,1024,1024]{2,1,0:T(8,128)}) fusion(bf16[3,1024,128]{2,1,0:T(8,128)(2,1)} %get-tuple-element.195, bf16[8,1024,3,128]{3,1,2,0:T(8,128)(2,1)} %get-tuple-element.194, s32[]{:T(128)} %get-tuple-element.181), kind=kOutput, calls=%fused_computation.1.clone.1 | convolution fusion | flops 811594752 | bytes 14168576 | tf_op jit(solution)/shard_map/while/body/eval_jaxpr/hqd,khd->hqk/dot_general | solution.py:76
  571.4 6.8 fusion.41
  584.9 11.9 %bitcast_convert_fusion = bf16[1024,6144]{1,0:T(8,128)(2,1)} fusion(bf16[3,128,6144]{2,1,0:T(8,128)(2,1)} %all-gather.10.cloned.1.call-done, f32[3,1024,128]{2,1,0:T(8,128)} %get-tuple-element.43, f32[3,1024]{1,0:T(4,128)S(1)} %get-tuple-element.44), kind=kOutput, calls=%fused_computation.22 | convolution fusion | flops 4838916096 | bytes 18886656 | tf_op jit(solution)/shard_map/dot_general | solution.py:100
  596.8 123.1 %reduce-scatter.2.cloned.1.call-done = bf16[64,6144]{1,0:T(8,128)(2,1)} async-done(((bf16[1024,6144]{1,0:T(8,128)(2,1)}), bf16[64,6144]{1,0:T(8,128)(2,1)}) %reduce-scatter.2.cloned.1.call-update) | async-done | bytes 786448 | tf_op jit(solution)/shard_map/reduce_scatter | solution.py:99
  (91 shorter events, 51.2 us)
Async XLA Ops:
  6.5 3.7 copy-start
  6.5 104.4 %all-gather.6.cloned.1.call-start = ((), (), s32[]{:S(2)}) async-start(), calls=%async_computation.1 | async-start | bytes 13369344 | tf_op jit(solution)/shard_map/all_gather | solution.py:48
  15.8 0.7 copy-start.4
  17.7 18.9 %copy-start.5 = (f32[2,3,128]{2,0,1:T(2,128)S(1)}, f32[2,3,128]{2,0,1:T(2,128)}, u32[]{:S(2)}) copy-start(f32[2,3,128]{2,0,1:T(2,128)} %param.14) | copy-start | bytes 9220
  17.7 243.2 %all-gather.8.cloned.1.call-start = ((), (), s32[]{:S(2)}) async-start(), calls=%async_computation.2 | async-start | bytes 7077888 | tf_op jit(solution)/shard_map/all_gather | solution.py:64
  130.2 2.1 copy-start.3
  133.7 258.8 %all-gather.12.cloned.1.call-start = ((), (), s32[]{:S(2)}) async-start(), calls=%async_computation.5 | async-start | bytes 7077888 | tf_op jit(solution)/shard_map/all_gather | solution.py:65
  136.2 448.6 %all-gather.10.cloned.1.call-start = ((), (), s32[]{:S(2)}) async-start(), calls=%async_computation.3 | async-start | bytes 5308416 | tf_op jit(solution)/shard_map/all_gather | solution.py:96
  136.8 583.1 %reduce-scatter.2.cloned.1.call-start = ((), (), s32[]{:S(2)}) async-start(), calls=%async_computation.4 | async-start | bytes 13369344 | tf_op jit(solution)/shard_map/reduce_scatter | solution.py:99
  422.3 8.3 %copy-start.2 = (f32[3,1024,1024]{2,1,0:T(8,128)S(1)}, f32[3,1024,1024]{2,1,0:T(8,128)}, u32[]{:S(2)}) copy-start(f32[3,1024,1024]{2,1,0:T(8,128)} %get-tuple-element.169) | copy-start | bytes 37748740 | tf_op jit(solution)/shard_map/while
  443.5 8.3 %copy-start.2 = (f32[3,1024,1024]{2,1,0:T(8,128)S(1)}, f32[3,1024,1024]{2,1,0:T(8,128)}, u32[]{:S(2)}) copy-start(f32[3,1024,1024]{2,1,0:T(8,128)} %get-tuple-element.169) | copy-start | bytes 37748740 | tf_op jit(solution)/shard_map/while
  464.9 8.3 %copy-start.2 = (f32[3,1024,1024]{2,1,0:T(8,128)S(1)}, f32[3,1024,1024]{2,1,0:T(8,128)}, u32[]{:S(2)}) copy-start(f32[3,1024,1024]{2,1,0:T(8,128)} %get-tuple-element.169) | copy-start | bytes 37748740 | tf_op jit(solution)/shard_map/while
  486.3 8.2 %copy-start.2 = (f32[3,1024,1024]{2,1,0:T(8,128)S(1)}, f32[3,1024,1024]{2,1,0:T(8,128)}, u32[]{:S(2)}) copy-start(f32[3,1024,1024]{2,1,0:T(8,128)} %get-tuple-element.169) | copy-start | bytes 37748740 | tf_op jit(solution)/shard_map/while
  507.5 8.2 %copy-start.2 = (f32[3,1024,1024]{2,1,0:T(8,128)S(1)}, f32[3,1024,1024]{2,1,0:T(8,128)}, u32[]{:S(2)}) copy-start(f32[3,1024,1024]{2,1,0:T(8,128)} %get-tuple-element.169) | copy-start | bytes 37748740 | tf_op jit(solution)/shard_map/while
  528.8 8.2 %copy-start.2 = (f32[3,1024,1024]{2,1,0:T(8,128)S(1)}, f32[3,1024,1024]{2,1,0:T(8,128)}, u32[]{:S(2)}) copy-start(f32[3,1024,1024]{2,1,0:T(8,128)} %get-tuple-element.169) | copy-start | bytes 37748740 | tf_op jit(solution)/shard_map/while
  550.1 8.2 %copy-start.2 = (f32[3,1024,1024]{2,1,0:T(8,128)S(1)}, f32[3,1024,1024]{2,1,0:T(8,128)}, u32[]{:S(2)}) copy-start(f32[3,1024,1024]{2,1,0:T(8,128)} %get-tuple-element.169) | copy-start | bytes 37748740 | tf_op jit(solution)/shard_map/while
  571.3 8.2 %copy-start.2 = (f32[3,1024,1024]{2,1,0:T(8,128)S(1)}, f32[3,1024,1024]{2,1,0:T(8,128)}, u32[]{:S(2)}) copy-start(f32[3,1024,1024]{2,1,0:T(8,128)} %get-tuple-element.169) | copy-start | bytes 37748740 | tf_op jit(solution)/shard_map/while
  596.8 123.1 %copy-start.1 = (bf16[8,8,768]{2,1,0:T(8,128)(2,1)S(1)}, bf16[8,8,768]{2,1,0:T(8,128)(2,1)}, u32[]{:S(2)}) copy-start(bf16[8,8,768]{2,1,0:T(8,128)(2,1)} %param.9) | copy-start | bytes 294916
Sparse Core Ops, SparseCore 0:
  17.8 93.0 all-gather.5
  133.9 127.0 all-gather.7
  262.6 129.9 all-gather.11
  394.1 100.9 all-gather.9
  596.9 122.9 reduce-scatter.1
where the time goes:
time: 728 us; the launch traced here: 726 us
  waiting for transfers between devices  431 us (59%)
  matrix products  141 us (19%)
  local copies, waits for them, and re-layouts  78.8 us (11%)
  other arithmetic  61.9 us (9%)
  between operations  13.3 us (2%)
    reduce_scatter x1, waiting for transfers between devices, local(): lax.psum_scatter(jnp.dot(context, out_weight, preferred_element_type=jnp....  123 us
    all_gather x1, waiting for transfers between devices, local(): key_piece = lax.all_gather(keys_here, 'row', axis=0, tiled=True)  123 us
    all_gather x1, waiting for transfers between devices, local(): value_piece = lax.all_gather(values_here, 'row', axis=0, tiled=True)  110 us
    all_gather x1, waiting for transfers between devices, local(): normed_piece = lax.all_gather(own_tile, 'col', axis=1, tiled=True)  74.4 us
    unnamed x17, local copies, waits for them, and re-layouts  65.4 us
    dot_general x8, matrix products, step_block(): jnp.einsum('hqd,khd->hqk', query_heads, block_keys, preferred_element_typ...  62 us
    reduce_sum x8, other arithmetic, step_block(): new_total = run_total * rescale + jnp.sum(exponent, axis=2)  54.5 us
    dot_general x8, matrix products, step_block(): jnp.einsum('hqk,khd->hqd', exponent.astype(jnp.bfloat16), block_values, p...  42.6 us
  transfers between devices with their start and end apart: 5, of which 4 were waited for; matrix products, arithmetic and copies ran while one was open for 31% of the time, Pallas kernels for 0%

commit v1 on v0

--- a/solution.py
+++ b/solution.py
@@ -45,7 +45,9 @@
     )
     normed = layer_norm(embedded, gain_row).astype(jnp.bfloat16)
     own_tile = normed.reshape(tile_rows, piece_cols, model_width)
-    normed_piece = lax.all_gather(own_tile, "col", axis=1, tiled=True)
+    normed_piece = jnp.concatenate(
+        lax.all_to_all(jnp.stack([own_tile] * lax.axis_size("col")), "col", 0, 0), axis=1
+    )
     piece_cols = normed_piece.shape[1]
     flat_normed = normed_piece.reshape(tile_rows * piece_cols, model_width)
     projected = jnp.dot(flat_normed, qkv_matrix, preferred_element_type=jnp.float32)

time: 728 us -> 865 us (1.19)
  waiting for transfers between devices: 431 us -> 535 us
  local copies, waits for them, and re-layouts: 78.8 us -> 98.2 us
  starting transfers between devices: 0.35 us -> 9.01 us
    all_to_all x0 -> x1, waiting for transfers between devices: none -> 168 us  [local(): lax.all_to_all(jnp.stack([own_tile] * lax.axis_size('col')), 'col', 0, 0)]
    all_gather x1 -> x0, waiting for transfers between devices: 74.4 us -> none  [local(): normed_piece = lax.all_gather(own_tile, 'col', axis=1, tiled=True)]
    reshape x0 -> x1, local copies, waits for them, and re-layouts: none -> 11.4 us  [local(): jnp.concatenate(lax.all_to_all(jnp.stack([own_tile] * lax.axis_size('col'...]
    all_gather x1, waiting for transfers between devices: 123 us -> 133 us  [local(): key_piece = lax.all_gather(keys_here, 'row', axis=0, tiled=True)]
    unnamed x17 -> x19, local copies, waits for them, and re-layouts: 65.4 us -> 67.2 us
  transfers between devices with their start and end apart: 5 -> 5, of which waited for: 4 -> 4; matrix products, arithmetic and copies ran while one was open for 31% -> 26% of each run, Pallas kernels for 0% -> 0%
where the time goes in v1:
time: 865 us; the launch traced here: 859 us
  waiting for transfers between devices  535 us (62%)
  matrix products  142 us (16%)
  local copies, waits for them, and re-layouts  98.2 us (11%)
  other arithmetic  61 us (7%)
  between operations  13.5 us (2%)
  starting transfers between devices  9.01 us (1%)
    all_to_all x1, waiting for transfers between devices, local(): lax.all_to_all(jnp.stack([own_tile] * lax.axis_size('col')), 'col', 0, 0)  168 us
    all_gather x1, waiting for transfers between devices, local(): key_piece = lax.all_gather(keys_here, 'row', axis=0, tiled=True)  133 us
    reduce_scatter x1, waiting for transfers between devices, local(): lax.psum_scatter(jnp.dot(context, out_weight, preferred_element_type=jnp....  123 us
    all_gather x1, waiting for transfers between devices, local(): value_piece = lax.all_gather(values_here, 'row', axis=0, tiled=True)  110 us
    unnamed x19, local copies, waits for them, and re-layouts  67.2 us
    dot_general x8, matrix products, step_block(): jnp.einsum('hqd,khd->hqk', query_heads, block_keys, preferred_element_typ...  61.7 us
    reduce_sum x8, other arithmetic, step_block(): new_total = run_total * rescale + jnp.sum(exponent, axis=2)  54.5 us
    dot_general x8, matrix products, step_block(): jnp.einsum('hqk,khd->hqd', exponent.astype(jnp.bfloat16), block_values, p...  42.6 us
  transfers between devices with their start and end apart: 5, of which 4 were waited for; matrix products, arithmetic and copies ran while one was open for 26% of the time, Pallas kernels for 0%

profile of v1, /device:TPU:0, one launch (start us, length us, event | category | flops | bytes accessed | tf_op | source)
XLA Modules:
  0.0 858.8 jit_solution(1056067448675297207)
XLA Ops:
  10.2 5.6 fusion.27
  16.8 6.1 stack.3
  22.9 8.0 all-to-all-start
  31.3 18.7 %copy.19 = bf16[6144,3,3,128]{0,3,2,1:T(8,128)(2,1)} copy(bf16[6144,3,3,128]{3,0,2,1:T(8,128)(2,1)} %param.13) | data formatting | bytes 28311552 | tf_op args[4]
  50.0 168.5 %all-to-all-done = bf16[16,8,8,6144]{3,2,1,0:T(8,128)(2,1)} async-done(((bf16[16,8,8,6144]{3,2,1,0:T(8,128)(2,1)}), bf16[16,8,8,6144]{3,2,1,0:T(8,128)(2,1)}, u32[]{:S(2)}, u32[]{:S(2)}) %all-to-all-start) | async-done | bytes 12582944 | tf_op jit(solution)/shard_map/all_to_all | solution.py:49
  218.5 11.4 %copy.18 = bf16[8,16,8,6144]{3,2,1,0:T(8,128)(2,1)} copy(bf16[8,16,8,6144]{3,2,0,1:T(8,128)(2,1)} %bitcast.2) | data formatting | bytes 25165824 | tf_op jit(solution)/shard_map/reshape | solution.py:48
  231.9 20.3 %fusion.19 = f32[1024,3,3,128]{0,3,2,1:T(8,128)S(1)} fusion(bf16[1024,6144,1,1]{1,0,3,2:T(8,128)(2,1)} %bitcast.96, bf16[6144,3,3,128]{0,3,2,1:T(8,128)(2,1)S(1)} %copy-done.4), kind=kOutput, calls=%fused_computation.23 | convolution fusion | flops 14495514624 | bytes 31457280 | tf_op jit(solution)/shard_map/dot_general | solution.py:53
  260.7 132.7 %all-gather.5.cloned.1.call-done = bf16[8192,3,128]{0,2,1:T(8,128)(2,1)} async-done(((bf16[1024,3,128]{0,2,1:T(8,128)(2,1)}), bf16[8192,3,128]{0,2,1:T(8,128)(2,1)}) %all-gather.5.cloned.1.call-update) | async-done | bytes 6291472 | tf_op jit(solution)/shard_map/all_gather | solution.py:66
  393.4 12.6 %copy.27 = bf16[48,8,8,1024]{3,2,1,0:T(8,128)(2,1)} copy(bf16[48,8,8,1024]{3,1,2,0:T(8,128)(2,1)} %bitcast.97) | data formatting | bytes 12582912
  406.1 9.3 %copy.20 = bf16[8,1024,3,128]{3,1,2,0:T(8,128)(2,1)} copy(bf16[8,1024,3,128]{1,0,3,2:T(8,128)(2,1)} %bitcast.94) | data formatting | bytes 12582912
  415.3 109.7 %all-gather.9.cloned.1.call-done = bf16[8192,1,3,128]{0,3,2,1:T(8,128)(2,1)} async-done(((bf16[1024,1,3,128]{0,3,2,1:T(8,128)(2,1)}), bf16[8192,1,3,128]{0,3,2,1:T(8,128)(2,1)}) %all-gather.9.cloned.1.call-update) | async-done | bytes 6291472 | tf_op jit(solution)/shard_map/all_gather | solution.py:67
  525.0 12.7 %copy.28 = bf16[48,8,8,1024]{3,2,1,0:T(8,128)(2,1)} copy(bf16[48,8,8,1024]{3,1,2,0:T(8,128)(2,1)} %bitcast.98) | data formatting | bytes 12582912
  537.7 9.1 %copy.22 = bf16[8,1024,3,128]{3,1,2,0:T(8,128)(2,1)} copy(bf16[8,1024,3,128]{1,0,3,2:T(8,128)(2,1)} %bitcast.95) | data formatting | bytes 12582912
  546.8 170.2 %while.15 = (s32[]{:T(128)}, f32[3,1024]{1,0:T(4,128)S(1)}, f32[3,1024]{1,0:T(4,128)S(1)}, f32[3,1024,128]{2,1,0:T(8,128)}, bf16[8,1024,3,128]{3,1,2,0:T(8,128)(...) while((s32[]{:T(128)}, f32[3,1024]{1,0:T(4,128)S(1)}, ...), condition=%wide.region_9.10_spmd.clone, body=%wide.region_6.9_spmd.clone.sunk | while | flops 1636973568 | bytes 93783168 | solution.py:94
  547.0 7.7 bitcast_reduce_fusion.2
  554.8 6.9 fusion.41
  568.2 7.7 bitcast_reduce_fusion.2
  575.9 6.8 fusion.41
  589.5 7.7 bitcast_reduce_fusion.2
  597.3 6.8 fusion.41
  610.9 7.7 bitcast_reduce_fusion.2
  618.6 6.8 fusion.41
  632.1 7.7 bitcast_reduce_fusion.2
  639.9 6.8 fusion.41
  653.4 7.7 bitcast_reduce_fusion.2
  661.1 6.8 fusion.41
  674.6 7.7 bitcast_reduce_fusion.2
  682.3 6.8 fusion.41
  695.8 7.7 bitcast_reduce_fusion.2
  703.6 6.8 fusion.41
  717.1 11.8 %bitcast_convert_fusion = bf16[1024,6144]{1,0:T(8,128)(2,1)} fusion(bf16[3,128,6144]{2,1,0:T(8,128)(2,1)} %all-gather.7.cloned.1.call-done, f32[3,1024,128]{2,1,0:T(8,128)} %get-tuple-element.43, f32[3,1024]{1,0:T(4,128)S(1)} %get-tuple-element.44), kind=kOutput, calls=%fused_computation.22 | convolution fusion | flops 4838916096 | bytes 18886656 | tf_op jit(solution)/shard_map/dot_general | solution.py:102
  728.9 123.1 %reduce-scatter.2.cloned.1.call-done = bf16[64,6144]{1,0:T(8,128)(2,1)} async-done(((bf16[1024,6144]{1,0:T(8,128)(2,1)}), bf16[64,6144]{1,0:T(8,128)(2,1)}) %reduce-scatter.2.cloned.1.call-update) | async-done | bytes 786448 | tf_op jit(solution)/shard_map/reduce_scatter | solution.py:101
  (94 shorter events, 69.1 us)
Async XLA Ops:
  6.5 3.7 copy-start
  15.8 0.7 copy-start.5
  22.9 195.6 %all-to-all-start = ((bf16[16,8,8,6144]{3,2,1,0:T(8,128)(2,1)}), bf16[16,8,8,6144]{3,2,1,0:T(8,128)(2,1)}, u32[]{:S(2)}, u32[]{:S(2)}) async-start(bf16[16,8,8,6144]{3,2,1,0:T(8,128)(2,1)} %stack.3), calls=%async_computation | async-start | bytes 25165824 | tf_op jit(solution)/shard_map/all_to_all | solution.py:49
  31.0 19.1 %copy-start.6 = (f32[2,3,128]{2,0,1:T(2,128)S(1)}, f32[2,3,128]{2,0,1:T(2,128)}, u32[]{:S(2)}) copy-start(f32[2,3,128]{2,0,1:T(2,128)} %param.14) | copy-start | bytes 9220
  31.0 362.4 %all-gather.5.cloned.1.call-start = ((), (), s32[]{:S(2)}) async-start(), calls=%async_computation.2 | async-start | bytes 7077888 | tf_op jit(solution)/shard_map/all_gather | solution.py:66
  218.5 13.4 %copy-start.4 = (bf16[6144,3,3,128]{0,3,2,1:T(8,128)(2,1)S(1)}, bf16[6144,3,3,128]{0,3,2,1:T(8,128)(2,1)}, u32[]{:S(2)}) copy-start(bf16[6144,3,3,128]{0,3,2,1:T(8,128)(2,1)} %copy.19) | copy-start | bytes 42467332
  252.2 2.1 copy-start.3
  255.8 269.3 %all-gather.9.cloned.1.call-start = ((), (), s32[]{:S(2)}) async-start(), calls=%async_computation.5 | async-start | bytes 7077888 | tf_op jit(solution)/shard_map/all_gather | solution.py:67
  258.2 458.8 %all-gather.7.cloned.1.call-start = ((), (), s32[]{:S(2)}) async-start(), calls=%async_computation.3 | async-start | bytes 5308416 | tf_op jit(solution)/shard_map/all_gather | solution.py:98
  259.0 593.1 %reduce-scatter.2.cloned.1.call-start = ((), (), s32[]{:S(2)}) async-start(), calls=%async_computation.4 | async-start | bytes 13369344 | tf_op jit(solution)/shard_map/reduce_scatter | solution.py:101
  554.8 8.3 copy-start.2
  575.9 8.3 copy-start.2
  597.3 8.3 copy-start.2
  618.6 8.2 copy-start.2
  639.9 8.2 copy-start.2
  661.1 8.2 copy-start.2
  682.3 8.2 copy-start.2
  703.5 8.2 copy-start.2
  728.9 123.1 %copy-start.1 = (bf16[8,8,768]{2,1,0:T(8,128)(2,1)S(1)}, bf16[8,8,768]{2,1,0:T(8,128)(2,1)}, u32[]{:S(2)}) copy-start(bf16[8,8,768]{2,1,0:T(8,128)(2,1)} %param.9) | copy-start | bytes 294916
Sparse Core Ops, SparseCore 0:
  255.9 137.4 all-gather.4
  395.1 129.9 all-gather.8
  526.7 100.9 all-gather.6
  729.0 122.9 reduce-scatter.1
